TPU v7x, 32 devices: a whole 2x2x4 slice. The times are simulated.
32 devices in a mesh: pts: 16 (over z, y, core), cen: 2 (over x).
Axes of the slice: x: 2, y: 2, z: 4, core: 2. Of those that a mesh axis runs over, the one named last changes fastest.
Arguments:
- points: bfloat16 [4096, 256], P('pts'), may hold values from -64 to 64
- centroids: bfloat16 [65536, 256], P('cen'), may hold values from -10 to 10
Outputs:
- updated: float32 [65536, 256], P(('cen', 'pts'))
- log_norm: float32 [4096], P('pts')
All inputs are finite; a program needn't handle non-finite values.
Results may differ from a plain program's by a relative error of at most 0.0017.
Values may be sent and summed in bfloat16 or wider, within the bound.
A program may use at most 128 MiB of HBM per device.

v0:
```python
import jax
import jax.numpy as jnp
from jax import lax
from jax.sharding import PartitionSpec as P

inv_temp = 0.0625
prior_count = 1.0


def score_rows(rows, table, table_norms):
    products = lax.dot_general(
        rows, table, (((1,), (1,)), ((), ())), preferred_element_type=jnp.float32
    )
    return (2.0 * products - table_norms[None, :]) * inv_temp


def body(points, centroids):
    group_size = lax.axis_size("pts")
    group_index = lax.axis_index("pts")
    center_norms = jnp.sum(jnp.square(centroids.astype(jnp.float32)), axis=1)
    logits = score_rows(points, centroids, center_norms)
    local_peak = jnp.max(logits, axis=1)
    row_peak = lax.pmax(local_peak, "cen")
    row_total = lax.psum(jnp.sum(jnp.exp(logits - row_peak[:, None]), axis=1), "cen")
    log_norm = row_peak + jnp.log(row_total)
    owned = centroids.shape[0] // group_size
    own_centers = lax.dynamic_slice_in_dim(centroids, group_index * owned, owned, 0)
    own_norms = lax.dynamic_slice_in_dim(center_norms, group_index * owned, owned, 0)
    every_norm = lax.all_gather(log_norm, "pts", axis=0, tiled=True)
    segment = lax.all_gather(points, "pts", axis=0, tiled=True)
    again = score_rows(segment, own_centers, own_norms)
    rows_used = jnp.exp(again - every_norm[:, None]).astype(jnp.bfloat16)
    weighted = lax.dot_general(
        rows_used, segment, (((0,), (0,)), ((), ())), preferred_element_type=jnp.float32
    )
    masses = jnp.sum(rows_used.astype(jnp.float32), axis=0)
    weighted, masses = (weighted, masses)
    updated = (own_centers.astype(jnp.float32) + weighted) / (prior_count + masses)[:, None]
    return (updated, log_norm)


def solution(mesh):
    placed = (P("pts", None), P("cen", None))
    return jax.shard_map(
        body,
        mesh=mesh,
        in_specs=placed,
        out_specs=(P(("cen", "pts"), None), P("pts")),
        check_vma=False,
    )
```

profile of v0, /device:TPU:0, one launch (start us, length us, event | category | flops | bytes accessed | tf_op | source)
XLA Modules:
  0.0 120.5 jit_solution(12697946490426230266)
XLA Ops:
  7.2 0.0 copy-start.1
  7.2 0.0 all-gather.3.cloned.1.call-start
  7.2 0.7 all-gather.3.cloned.1.call-update
  7.9 7.6 %multiply_reduce_fusion = f32[32768]{0:T(1024)S(1)} fusion(bf16[32768,256]{1,0:T(8,128)(2,1)} %param.3), kind=kLoop, calls=%fused_computation.6 | loop fusion | flops 25133056 | bytes 16908288 | tf_op jit(solution)/shard_map/reduce_sum | solution.py:20
  15.5 0.0 copy-start
  15.5 0.0 copy-done.1
  15.5 24.6 %fusion.5 = (f32[256]{0:T(256)S(1)}, f32[256,32768]{1,0:T(8,128)}) fusion(f32[32768]{0:T(1024)S(1)} %multiply_reduce_fusion, bf16[256,256]{1,0:T(8,128)(2,1)S(1)} %copy-done.1, bf16[32768,256]{1,0:T(8,128)(2,1)} %param.3), kind=kOutput, calls=%fused_computation.13 | convolution fusion | flops 4328521728 | bytes 50594816 | tf_op jit(solution)/shard_map/dot_general | solution.py:11
  40.2 0.0 copy-done
  40.2 5.9 %pmax.7 = f32[256]{0:T(256)S(1)} all-reduce(f32[256]{0:T(256)S(1)} %get-tuple-element.2), channel_id=1, replica_groups=mesh['pts'=16,'cen'=2] {'cen'}, use_global_device_ids=true, to_apply=%region_2.0 | all-reduce | flops 256 | bytes 2048 | tf_op jit(solution)/shard_map/pmax | solution.py:23
  46.0 0.0 dynamic-slice-start
  46.0 13.8 %exponential_reduce_fusion = f32[256]{0:T(256)S(1)} fusion(f32[256,32768]{1,0:T(8,128)} %get-tuple-element.3, f32[256]{0:T(256)S(1)} %pmax.7), kind=kLoop, calls=%fused_computation.5 | loop fusion | flops 16776960 | bytes 33556480 | tf_op jit(solution)/shard_map/reduce_sum | solution.py:24
  59.8 4.9 %psum.7 = f32[256]{0:T(256)S(1)} all-reduce(f32[256]{0:T(256)S(1)} %exponential_reduce_fusion), channel_id=1, replica_groups=mesh['pts'=16,'cen'=2] {'cen'}, use_global_device_ids=true, to_apply=%region_4.0 | all-reduce | flops 256 | bytes 2048 | tf_op jit(solution)/shard_map/psum | solution.py:24
  64.7 0.0 copy-start.2
  64.7 22.4 %all-gather = f32[16,1,256]{2,1,0:T(1,128)S(1)} all-gather(f32[1,1,256]{2,1,0:T(1,128)S(1)} %bitcast.8), channel_id=1, replica_groups=mesh['pts'=16,'cen'=2] {'pts'}, dimensions={0}, use_global_device_ids=true | all-gather | bytes 17408 | tf_op jit(solution)/shard_map/all_gather | solution.py:29
  87.1 0.0 all-gather.3.cloned.1.call-done
  87.1 0.0 dynamic-slice-done
  87.1 0.0 copy-start.3
  87.1 14.3 %convert_reduce_fusion = (f32[2048]{0:T(1024)S(1)}, bf16[2048,4096]{1,0:T(8,128)(2,1)}) fusion(f32[4096]{0:T(1024)S(1)} %bitcast.7, f32[2048]{0:T(1024)S(1)} %dynamic-slice-done, bf16[4096,256]{1,0:T(8,128)(2,1)} %all-gather.3.cloned.1.call-done, bf16[32768,256]{1,0:T(8,128)(2,1)} %param.3, s32[]{:T(128)} %select_n.4), kind=kOutput, calls=%fused_computation.3 | convolution fusion | flops 4353685504 | bytes 19956224 | tf_op jit(solution)/shard_map/dot_general | solution.py:11
  101.4 0.0 copy-done.2
  101.4 0.0 copy-done.3
  101.4 12.2 %fusion.2 = f32[2048,256]{1,0:T(8,128)} fusion(bf16[2048,4096]{1,0:T(8,128)(2,1)} %get-tuple-element.5, bf16[4096,256]{1,0:T(8,128)(2,1)S(1)} %copy-done.3, f32[2048]{0:T(1024)S(1)} %broadcast_add_fusion, bf16[32768,256]{1,0:T(8,128)(2,1)} %param.3, s32[]{:T(128)} %select_n.4), kind=kOutput, calls=%fused_computation.8 | convolution fusion | flops 4296540160 | bytes 22028292 | tf_op jit(solution)/shard_map/dot_general | solution.py:33
  (2 shorter events, 0.0 us)
Async XLA Ops:
  7.2 8.4 %copy-start.1 = (bf16[256,256]{1,0:T(8,128)(2,1)S(1)}, bf16[256,256]{1,0:T(8,128)(2,1)}, u32[]{:S(2)}) copy-start(bf16[256,256]{1,0:T(8,128)(2,1)} %param.2) | copy-start | bytes 393220
  7.2 79.9 %all-gather.3.cloned.1.call-start = ((), (), s32[]{:S(2)}) async-start(), calls=%async_computation | async-start | bytes 2228224 | tf_op jit(solution)/shard_map/all_gather | solution.py:30
  15.5 24.7 %copy-start = (f32[32768]{0:T(1024)}, f32[32768]{0:T(1024)S(1)}, u32[]{:S(2)}) copy-start(f32[32768]{0:T(1024)S(1)} %multiply_reduce_fusion) | copy-start | bytes 393220
  46.0 41.1 %dynamic-slice-start = ((f32[32768]{0:T(1024)}, s32[]{:T(128)}), f32[2048]{0:T(1024)S(1)}, s32[]{:S(2)}) async-start(f32[32768]{0:T(1024)} %copy-done, s32[]{:T(128)} %select_n.4), calls=%async_computation.1 | async-start | bytes 16896 | tf_op jit(solution)/shard_map/dynamic_slice | solution.py:28
  64.7 36.6 %copy-start.2 = (f32[256]{0:T(256)}, f32[256]{0:T(256)S(1)}, u32[]{:S(2)}) copy-start(f32[256]{0:T(256)S(1)} %log_add_fusion) | copy-start | bytes 3076
  87.1 14.3 %copy-start.3 = (bf16[4096,256]{1,0:T(8,128)(2,1)S(1)}, bf16[4096,256]{1,0:T(8,128)(2,1)}, u32[]{:S(2)}) copy-start(bf16[4096,256]{1,0:T(8,128)(2,1)} %all-gather.3.cloned.1.call-done) | copy-start | bytes 6291460
Sparse Core Ops, SparseCore 0:
  10.1 44.1 all-gather.2
where the time goes:
time: 121 us; the launch traced here: 120 us
  matrix products  51.1 us (42%)
  blocking collectives  33.2 us (27%)
  other arithmetic  21.4 us (18%)
  between operations  14.1 us (12%)
    dot_general x2, matrix products, score_rows(): lax.dot_general(rows, table, (((1,), (1,)), ((), ())), preferred_element_...  38.9 us
    all_gather x1, blocking collectives, body(): every_norm = lax.all_gather(log_norm, 'pts', axis=0, tiled=True)  22.4 us
    reduce_sum x1, other arithmetic, body(): jnp.sum(jnp.exp(logits - row_peak[:, None]), axis=1)  13.8 us
    dot_general x1, matrix products, body(): lax.dot_general(rows_used, segment, (((0,), (0,)), ((), ())), preferred_e...  12.2 us
    reduce_sum x1, other arithmetic, body(): center_norms = jnp.sum(jnp.square(centroids.astype(jnp.float32)), axis=1)  7.59 us
    pmax x1, blocking collectives, body(): row_peak = lax.pmax(local_peak, 'cen')  5.86 us
    psum x1, blocking collectives, body(): lax.psum(jnp.sum(jnp.exp(logits - row_peak[:, None]), axis=1), 'cen')  4.93 us
  transfers between devices with their start and end apart: 1, of which 0 were waited for; matrix products, arithmetic and copies ran while one was open for 38% of the time, Pallas kernels for 0%

commit v1 on v0

v1 whole, which is shorter than its diff:
```python
import functools
import math

import jax
import jax.numpy as jnp
from jax import lax
from jax.experimental import pallas as pl
from jax.experimental.pallas import tpu as pltpu
from jax.sharding import PartitionSpec as P

inv_temp = 0.0625
prior_count = 1.0
log2e = math.log2(math.e)
MESH = pl.DeviceIdType.MESH


def kernel(
    G, C, points_ref, table_ref, out_ref, norm_ref,
    pts_all, pts_scaled, table, half_norms, scores, shares,
    peaks, local_log, all_local, every_norm, factors,
    load_sem, send_sem, ring_sem, twin_sem, stat_send, stat_recv, norm_send, norm_recv,
):
    T, D = points_ref.shape
    own = table.shape[0]
    R = G // 2
    far = R // 2
    half = T // 2
    N = G * C
    RB = min(256, own)
    NB = own // RB
    me = lax.axis_index("pts")
    cen = lax.axis_index("cen")
    mine = cen * G + me
    core = me % 2
    chip = me // 2
    turn = chip % 2
    pos = (chip // 2) * (1 - turn) + (R - 1 - chip // 2) * turn

    def tile_at(p, c):
        s = p // far
        return ((1 - s) * 2 * p + s * (2 * (R - 1 - p) + 1)) * 2 + c

    twin = me + 1 - 2 * core
    right = tile_at((pos + 1) % R, core)
    left = tile_at((pos + R - 1) % R, core)

    my_points = pts_all.at[pl.ds(pl.multiple_of(me * T, T), T)]
    load_points = pltpu.make_async_copy(points_ref, my_points, load_sem.at[0])
    load_points.start()
    load_table = pltpu.make_async_copy(
        table_ref.at[pl.ds(pl.multiple_of(me * own, own), own)], table, load_sem.at[1]
    )
    load_table.start()

    barrier = pltpu.get_barrier_semaphore()

    def greet(i, carry):
        @pl.when(i != mine)
        def _():
            pl.semaphore_signal(
                barrier, inc=1, device_id={"pts": i % G, "cen": i // G}, device_id_type=MESH
            )
        return carry

    lax.fori_loop(0, N, greet, 0)
    load_points.wait()
    pl.semaphore_wait(barrier, N - 1)

    def rows_of(t, h):
        return pts_all.at[pl.ds(pl.multiple_of(t * T + h * half, half), half)]

    def from_left(d):
        return tile_at((pos + R - d) % R, core)

    def from_right(d):
        return tile_at((pos + d) % R, core)

    def ring_copy(way, d, h, t):
        return pltpu.make_async_remote_copy(
            src_ref=rows_of(t, h), dst_ref=rows_of(t, h), send_sem=send_sem,
            recv_sem=ring_sem.at[way, d, h],
            device_id={"pts": (right, left)[way], "cen": cen}, device_id_type=MESH,
        )

    def twin_copy(way, d, h, t):
        return pltpu.make_async_remote_copy(
            src_ref=rows_of(t, h), dst_ref=rows_of(t, h), send_sem=send_sem,
            recv_sem=twin_sem.at[way, d, h],
            device_id={"pts": twin, "cen": cen}, device_id_type=MESH,
        )

    for h in range(2):
        ring_copy(0, 1, h, me).start()
        ring_copy(1, 1, 1 - h, me).start()
    for h in range(2):
        twin_copy(0, 0, h, me).start()

    load_table.wait()

    def norms(r, carry):
        rows = pl.ds(pl.multiple_of(r * RB, RB), RB)
        block = table[rows, :].astype(jnp.float32)
        total = jnp.sum(block * block, axis=1, keepdims=True)
        half_norms[rows, :] = jnp.broadcast_to(0.5 * total, (RB, T))
        return carry

    lax.fori_loop(0, NB, norms, 0)

    def process(t):
        cols = pl.ds(pl.multiple_of(t * T, T), T)
        tile = pts_all[cols, :]

        def score(r, top):
            rows = pl.ds(pl.multiple_of(r * RB, RB), RB)
            u = lax.dot_general(
                table[rows, :], tile, (((1,), (1,)), ((), ())),
                preferred_element_type=jnp.float32,
            ) - half_norms[rows, :]
            scores[rows, :] = u
            return jnp.maximum(top, jnp.max(u.reshape(RB // 8, 8, T), axis=0))

        top = lax.fori_loop(
            0, NB, score, jnp.full((8, T), -jnp.inf, jnp.float32), unroll=True
        )
        peak = jnp.max(top, axis=0, keepdims=True)

        def weigh(r, total):
            rows = pl.ds(pl.multiple_of(r * RB, RB), RB)
            e = jnp.exp2((scores[rows, :] - peak) * (2.0 * inv_temp * log2e))
            shares[rows, cols] = e.astype(jnp.bfloat16)
            return total + jnp.sum(e.reshape(RB // 8, 8, T), axis=0)

        total = lax.fori_loop(0, NB, weigh, jnp.zeros((8, T), jnp.float32), unroll=True)
        scaled_peak = peak * (2.0 * inv_temp)
        peaks[t] = scaled_peak
        value = scaled_peak + jnp.log(jnp.sum(total, axis=0, keepdims=True))
        local_log[t] = value

        @pl.when(t == me)
        def _():
            all_local[mine] = value

        def tell(c, carry):
            @pl.when(c * G + t != mine)
            def _():
                pltpu.make_async_remote_copy(
                    src_ref=local_log.at[t], dst_ref=all_local.at[mine],
                    send_sem=stat_send, recv_sem=stat_recv,
                    device_id={"pts": t, "cen": c}, device_id_type=MESH,
                ).start()
            return carry

        lax.fori_loop(0, C, tell, 0)

    other = 1 - 2 * core

    def twin_ready(way, d, t):
        for h in range(2):
            twin_copy(way, d, h, t).wait_recv()

    process(me)

    def step(d, carry):
        a, b = from_left(d), from_right(d)

        def pass_on(h0, h1):
            for way, h, t in ((0, h0, a), (1, h1, b)):
                ring_copy(way, d, h, t).wait_recv()

                @pl.when((d + 1 < far) | (h == way))
                def _():
                    ring_copy(way, d + 1, h, t).start()

                twin_copy(way, d, h, t).start()

        pass_on(0, 1)
        la, lb = from_left(d - 1) + other, from_right(d - 1) + other

        def earlier(k, carry):
            @pl.when(k == 0)
            def _():
                twin_ready(0, d - 1, la)

            @pl.when(k == 1)
            def _():
                twin_ready(1, d - 1, lb)

            process(la * (1 - k) + lb * k)
            return carry

        lax.fori_loop(0, jnp.minimum(d, 2), earlier, 0)
        pass_on(1, 0)

        def now(k, carry):
            process(a * (1 - k) + b * k)
            return carry

        lax.fori_loop(0, 2, now, 0)
        return carry

    lax.fori_loop(1, far, step, 0)

    last = from_left(far)
    for way in range(2):
        ring_copy(way, far, way, last).wait_recv()
        twin_copy(way, far, way, last).start()
    twin_ready(0, far - 1, from_left(far - 1) + other)
    twin_ready(1, far - 1, from_right(far - 1) + other)

    def tail(k, carry):
        @pl.when(k == 3)
        def _():
            for way in range(2):
                twin_copy(way, far, way, last + other).wait_recv()

        t = tile_at((pos + jnp.where(k == 0, R - far + 1, jnp.where(k == 1, far - 1, far))) % R, core)
        process(t + jnp.where(k == 2, 0, other))
        return carry

    lax.fori_loop(0, 4, tail, 0)

    pltpu.make_async_copy(
        all_local.at[pl.ds(0, N - 1)], all_local.at[pl.ds(0, N - 1)], stat_recv
    ).wait()
    logs = all_local[...].reshape(N, T)
    crest = jnp.max(logs, axis=0, keepdims=True)
    log_norm = crest + jnp.log(jnp.sum(jnp.exp(logs - crest), axis=0, keepdims=True))
    every_norm[me] = log_norm
    norm_ref[...] = log_norm

    def publish(i, carry):
        peer = (me + i) % G
        pltpu.make_async_remote_copy(
            src_ref=every_norm.at[me], dst_ref=every_norm.at[me],
            send_sem=norm_send, recv_sem=norm_recv,
            device_id={"pts": peer, "cen": cen}, device_id_type=MESH,
        ).start()
        return carry

    lax.fori_loop(1, G, publish, 0)
    group = every_norm.at[pl.ds(0, G - 1)]
    pltpu.make_async_copy(group, group, norm_recv).wait()

    def scale(t, carry):
        cols = pl.ds(pl.multiple_of(t * T, T), T)
        factor = jnp.exp(peaks[t] - every_norm[t])
        factors[:, cols] = jnp.broadcast_to(factor, (8, T))
        column = jnp.broadcast_to(factor, (8, T)).T[:, :1]
        pts_scaled[cols, :] = (pts_all[cols, :].astype(jnp.float32) * column).astype(jnp.bfloat16)
        return carry

    lax.fori_loop(0, G, scale, 0, unroll=2)

    KC = min(16, G)

    def update(r, carry):
        rows = pl.ds(pl.multiple_of(r * RB, RB), RB)

        def chunk(j, sums):
            weighted, mass = sums
            base = pl.multiple_of(j * KC * T, KC * T)
            weighted += jnp.dot(
                shares[rows, pl.ds(base, KC * T)], pts_scaled[pl.ds(base, KC * T), :],
                preferred_element_type=jnp.float32,
            )
            for k in range(KC):
                cols = pl.ds(pl.multiple_of(base + k * T, T), T)
                mass += jnp.sum(
                    (shares[rows, cols].astype(jnp.float32) * factors[:1, cols]).reshape(RB, T // 128, 128),
                    axis=1,
                )
            return weighted, mass

        start = (jnp.zeros((RB, D), jnp.float32), jnp.zeros((RB, 128), jnp.float32))
        weighted, mass = lax.fori_loop(0, G // KC, chunk, start, unroll=True)
        total = prior_count + jnp.sum(mass, axis=1, keepdims=True)
        out_ref[rows, :] = (table[rows, :].astype(jnp.float32) + weighted) / total
        return carry

    lax.fori_loop(0, NB, update, 0)

    sent = pts_all.at[pl.ds(0, (G - 1) * T)]
    pltpu.make_async_copy(sent, sent, send_sem).wait()
    pltpu.make_async_copy(
        all_local.at[pl.ds(0, N - 1)], all_local.at[pl.ds(0, N - 1)], stat_send
    ).wait()
    pltpu.make_async_copy(group, group, norm_send).wait()


def body(G, C, points, centroids):
    T, D = points.shape
    own = centroids.shape[0] // G
    far = G // 4
    updated, log_norm = pl.pallas_call(
        functools.partial(kernel, G, C),
        out_shape=(
            jax.ShapeDtypeStruct((own, D), jnp.float32),
            jax.ShapeDtypeStruct((1, T), jnp.float32),
        ),
        in_specs=[pl.BlockSpec(memory_space=pl.ANY)] * 2,
        out_specs=(pl.BlockSpec(memory_space=pltpu.VMEM),) * 2,
        scratch_shapes=[
            pltpu.VMEM((G * T, D), jnp.bfloat16),
            pltpu.VMEM((G * T, D), jnp.bfloat16),
            pltpu.VMEM((own, D), jnp.bfloat16),
            pltpu.VMEM((own, T), jnp.float32),
            pltpu.VMEM((own, T), jnp.float32),
            pltpu.VMEM((own, G * T), jnp.bfloat16),
            pltpu.VMEM((G, 1, T), jnp.float32),
            pltpu.VMEM((G, 1, T), jnp.float32),
            pltpu.VMEM((G * C, 1, T), jnp.float32),
            pltpu.VMEM((G, 1, T), jnp.float32),
            pltpu.VMEM((8, G * T), jnp.float32),
            pltpu.SemaphoreType.DMA((2,)),
            pltpu.SemaphoreType.DMA,
            pltpu.SemaphoreType.DMA((2, far + 1, 2)),
            pltpu.SemaphoreType.DMA((2, far + 1, 2)),
            pltpu.SemaphoreType.DMA,
            pltpu.SemaphoreType.DMA,
            pltpu.SemaphoreType.DMA,
            pltpu.SemaphoreType.DMA,
        ],
        compiler_params=pltpu.CompilerParams(
            collective_id=0, has_side_effects=True, vmem_limit_bytes=60 * 1024 * 1024
        ),
    )(points, centroids)
    return updated, log_norm.reshape(T)


def solution(mesh):
    placed = (P("pts", None), P("cen", None))
    return jax.shard_map(
        functools.partial(body, mesh.shape["pts"], mesh.shape["cen"]),
        mesh=mesh,
        in_specs=placed,
        out_specs=(P(("cen", "pts"), None), P("pts")),
        check_vma=False,
    )
```

time: 121 us -> 91.8 us (0.76)
  Pallas kernels: 0 us -> 87.4 us
  matrix products: 51.1 us -> 0 us
  blocking collectives: 33.2 us -> 0 us
  other arithmetic: 21.4 us -> 0 us
  between operations: 14.1 us -> 0.65 us
  local copies, waits for them, and re-layouts: 0.02 us -> 3.61 us
    pallas_call x0 -> x1, Pallas kernels: none -> 87.4 us  [body(): pl.pallas_call(functools.partial(kernel, G, C), out_shape=(jax.ShapeDtype...]
    dot_general x3 -> x0, matrix products: 51.1 us -> none  [the longest x2 38.9 us: score_rows(): lax.dot_general(rows, table, (((1,), (1,)), ((), ())), preferred_element_...]
    all_gather x1 -> x0, blocking collectives: 22.4 us -> none  [body(): every_norm = lax.all_gather(log_norm, 'pts', axis=0, tiled=True)]
    reduce_sum x2 -> x0, other arithmetic: 21.4 us -> none  [the longest x1 13.8 us: body(): jnp.sum(jnp.exp(logits - row_peak[:, None]), axis=1)]
    pmax x1 -> x0, blocking collectives: 5.86 us -> none  [body(): row_peak = lax.pmax(local_peak, 'cen')]
    psum x1 -> x0, blocking collectives: 4.93 us -> none  [body(): lax.psum(jnp.sum(jnp.exp(logits - row_peak[:, None]), axis=1), 'cen')]
    unnamed x8 -> x4, local copies, waits for them, and re-layouts: 0.02 us -> 3.61 us
  transfers between devices with their start and end apart: 1 -> 0, of which waited for: 0 -> 0; matrix products, arithmetic and copies ran while one was open for 38% -> 0% of each run, Pallas kernels for 0% -> 0%
where the time goes in v1:
time: 91.8 us; the launch traced here: 91.6 us
  Pallas kernels  87.4 us (95%)
  local copies, waits for them, and re-layouts  3.61 us (4%)
    pallas_call x1, Pallas kernels, body(): pl.pallas_call(functools.partial(kernel, G, C), out_shape=(jax.ShapeDtype...  87.4 us
    unnamed x4, local copies, waits for them, and re-layouts  3.61 us

profile of v1, /device:TPU:0, one launch (start us, length us, event | category | flops | bytes accessed | tf_op | source)
XLA Modules:
  0.0 91.6 jit_solution(176007709905446380)
XLA Ops:
  0.6 87.4 %shard_map.41 = (f32[2048,256]{1,0:T(8,128)}, f32[1,256]{1,0:T(1,128)}) custom-call(bf16[256,256]{1,0:T(8,128)(2,1)} %points_ref.1, bf16[32768,256]{1,0:T(8,128)(2,1)} %table_ref.1), custom_call_target="tpu_custom_call" | custom-call | tf_op jit(solution)/shard_map/pallas_call | solution.py:294
  88.0 0.0 copy-start
  88.0 3.0 %copy.6 = f32[2048,256]{1,0:T(8,128)} copy(f32[2048,256]{1,0:T(8,128)} %get-tuple-element.8) | data formatting | bytes 4194304
  91.1 0.0 copy-done
  91.1 0.6 copy.7
Async XLA Ops:
  88.0 3.1 %copy-start = (f32[1,256]{1,0:T(1,128)S(1)}, f32[1,256]{1,0:T(1,128)}, u32[]{:S(2)}) copy-start(f32[1,256]{1,0:T(1,128)} %get-tuple-element.5) | copy-start | bytes 3076

commit v2 on v1

--- a/solution.py
+++ b/solution.py
@@ -265,10 +265,9 @@
             )
             for k in range(KC):
                 cols = pl.ds(pl.multiple_of(base + k * T, T), T)
-                mass += jnp.sum(
-                    (shares[rows, cols].astype(jnp.float32) * factors[:1, cols]).reshape(RB, T // 128, 128),
-                    axis=1,
-                )
+                part = shares[rows, cols].astype(jnp.float32) * factors[:1, cols]
+                for g in range(T // 128):
+                    mass += part[:, g * 128:(g + 1) * 128]
             return weighted, mass
 
         start = (jnp.zeros((RB, D), jnp.float32), jnp.zeros((RB, 128), jnp.float32))

time: 91.8 us -> 48.8 us (0.53)
  Pallas kernels: 87.4 us -> 44.4 us
    pallas_call x1, Pallas kernels: 87.4 us -> 44.4 us  [body(): pl.pallas_call(functools.partial(kernel, G, C), out_shape=(jax.ShapeDtype...]
where the time goes in v2:
time: 48.8 us; the launch traced here: 48.6 us
  Pallas kernels  44.4 us (91%)
  local copies, waits for them, and re-layouts  3.61 us (7%)
  between operations  0.65 us (1%)
    pallas_call x1, Pallas kernels, body(): pl.pallas_call(functools.partial(kernel, G, C), out_shape=(jax.ShapeDtype...  44.4 us
    unnamed x4, local copies, waits for them, and re-layouts  3.61 us

profile of v2, /device:TPU:0, one launch (start us, length us, event | category | flops | bytes accessed | tf_op | source)
XLA Modules:
  0.0 48.6 jit_solution(806380484010571350)
XLA Ops:
  0.6 44.4 %shard_map.41 = (f32[2048,256]{1,0:T(8,128)}, f32[1,256]{1,0:T(1,128)}) custom-call(bf16[256,256]{1,0:T(8,128)(2,1)} %points_ref.1, bf16[32768,256]{1,0:T(8,128)(2,1)} %table_ref.1), custom_call_target="tpu_custom_call" | custom-call | tf_op jit(solution)/shard_map/pallas_call | solution.py:293
  45.0 0.0 copy-start
  45.0 3.0 %copy.6 = f32[2048,256]{1,0:T(8,128)} copy(f32[2048,256]{1,0:T(8,128)} %get-tuple-element.8) | data formatting | bytes 4194304
  48.1 0.0 copy-done
  48.1 0.6 %copy.7 = f32[256]{0:T(256)} copy(f32[256]{0:T(256)S(1)} %bitcast.1) | data formatting | bytes 2048
Async XLA Ops:
  45.0 3.1 %copy-start = (f32[1,256]{1,0:T(1,128)S(1)}, f32[1,256]{1,0:T(1,128)}, u32[]{:S(2)}) copy-start(f32[1,256]{1,0:T(1,128)} %get-tuple-element.5) | copy-start | bytes 3076

commit v3 on v2

--- a/solution.py
+++ b/solution.py
@@ -54,17 +54,16 @@
 
     barrier = pltpu.get_barrier_semaphore()
 
-    def greet(i, carry):
-        @pl.when(i != mine)
-        def _():
-            pl.semaphore_signal(
-                barrier, inc=1, device_id={"pts": i % G, "cen": i // G}, device_id_type=MESH
-            )
-        return carry
-
-    lax.fori_loop(0, N, greet, 0)
+    for peer in (right, left, twin):
+        pl.semaphore_signal(
+            barrier, inc=1, device_id={"pts": peer, "cen": cen}, device_id_type=MESH
+        )
+    for i in range(1, C):
+        pl.semaphore_signal(
+            barrier, inc=1, device_id={"pts": me, "cen": (cen + i) % C}, device_id_type=MESH
+        )
     load_points.wait()
-    pl.semaphore_wait(barrier, N - 1)
+    pl.semaphore_wait(barrier, 2 + C)
 
     def rows_of(t, h):
         return pts_all.at[pl.ds(pl.multiple_of(t * T + h * half, half), half)]
@@ -293,7 +292,7 @@
     updated, log_norm = pl.pallas_call(
         functools.partial(kernel, G, C),
         out_shape=(
-            jax.ShapeDtypeStruct((own, D), jnp.float32),
+            pltpu.VMEM((own, D), jnp.float32),
             jax.ShapeDtypeStruct((1, T), jnp.float32),
         ),
         in_specs=[pl.BlockSpec(memory_space=pl.ANY)] * 2,

time: 48.8 us -> 43.8 us (0.90)
  Pallas kernels: 44.4 us -> 41.1 us
  local copies, waits for them, and re-layouts: 3.61 us -> 1.89 us
    pallas_call x1, Pallas kernels: 44.4 us -> 41.1 us  [body(): pl.pallas_call(functools.partial(kernel, G, C), out_shape=(pltpu.VMEM((ow...]
    unnamed x4, local copies, waits for them, and re-layouts: 3.61 us -> 1.89 us
where the time goes in v3:
time: 43.8 us; the launch traced here: 43.7 us
  Pallas kernels  41.1 us (94%)
  local copies, waits for them, and re-layouts  1.89 us (4%)
  between operations  0.65 us (1%)
    pallas_call x1, Pallas kernels, body(): pl.pallas_call(functools.partial(kernel, G, C), out_shape=(pltpu.VMEM((ow...  41.1 us
    unnamed x4, local copies, waits for them, and re-layouts  1.89 us

profile of v3, /device:TPU:0, one launch (start us, length us, event | category | flops | bytes accessed | tf_op | source)
XLA Modules:
  0.0 43.7 jit_solution(655904776282974315)
XLA Ops:
  0.6 41.1 %shard_map.41 = (f32[2048,256]{1,0:T(8,128)S(1)}, f32[1,256]{1,0:T(1,128)}) custom-call(bf16[256,256]{1,0:T(8,128)(2,1)} %points_ref.1, bf16[32768,256]{1,0:T(8,128)(2,1)} %table_ref.1), custom_call_target="tpu_custom_call" | custom-call | tf_op jit(solution)/shard_map/pallas_call | solution.py:292
  41.8 0.0 copy-start
  41.8 1.3 %copy.6 = f32[2048,256]{1,0:T(8,128)} copy(f32[2048,256]{1,0:T(8,128)S(1)} %get-tuple-element.6) | data formatting | bytes 4194304
  43.1 0.0 copy-done
  43.1 0.6 %copy.7 = f32[256]{0:T(256)} copy(f32[256]{0:T(256)S(1)} %bitcast.1) | data formatting | bytes 2048
Async XLA Ops:
  41.8 1.3 %copy-start = (f32[1,256]{1,0:T(1,128)S(1)}, f32[1,256]{1,0:T(1,128)}, u32[]{:S(2)}) copy-start(f32[1,256]{1,0:T(1,128)} %get-tuple-element.5) | copy-start | bytes 3076

commit v4 on v3

--- a/solution.py
+++ b/solution.py
@@ -248,7 +248,7 @@
         pts_scaled[cols, :] = (pts_all[cols, :].astype(jnp.float32) * column).astype(jnp.bfloat16)
         return carry
 
-    lax.fori_loop(0, G, scale, 0, unroll=2)
+    lax.fori_loop(0, G, scale, 0, unroll=8)
 
     KC = min(16, G)
 
@@ -275,7 +275,7 @@
         out_ref[rows, :] = (table[rows, :].astype(jnp.float32) + weighted) / total
         return carry
 
-    lax.fori_loop(0, NB, update, 0)
+    lax.fori_loop(0, NB, update, 0, unroll=2 if NB % 2 == 0 else 1)
 
     sent = pts_all.at[pl.ds(0, (G - 1) * T)]
     pltpu.make_async_copy(sent, sent, send_sem).wait()

time: 43.8 us -> 42.8 us (0.977)
  Pallas kernels: 41.1 us -> 40.1 us
    pallas_call x1, Pallas kernels: 41.1 us -> 40.1 us  [body(): pl.pallas_call(functools.partial(kernel, G, C), out_shape=(pltpu.VMEM((ow...]
where the time goes in v4:
time: 42.8 us; the launch traced here: 42.6 us
  Pallas kernels  40.1 us (94%)
  local copies, waits for them, and re-layouts  1.89 us (4%)
  between operations  0.65 us (2%)
    pallas_call x1, Pallas kernels, body(): pl.pallas_call(functools.partial(kernel, G, C), out_shape=(pltpu.VMEM((ow...  40.1 us
    unnamed x4, local copies, waits for them, and re-layouts  1.89 us

profile of v4, /device:TPU:0, one launch (start us, length us, event | category | flops | bytes accessed | tf_op | source)
XLA Modules:
  0.0 42.6 jit_solution(2871812952010513966)
XLA Ops:
  0.6 40.1 %shard_map.41 = (f32[2048,256]{1,0:T(8,128)S(1)}, f32[1,256]{1,0:T(1,128)}) custom-call(bf16[256,256]{1,0:T(8,128)(2,1)} %points_ref.1, bf16[32768,256]{1,0:T(8,128)(2,1)} %table_ref.1), custom_call_target="tpu_custom_call" | custom-call | tf_op jit(solution)/shard_map/pallas_call | solution.py:292
  40.7 0.0 copy-start
  40.7 1.3 %copy.6 = f32[2048,256]{1,0:T(8,128)} copy(f32[2048,256]{1,0:T(8,128)S(1)} %get-tuple-element.6) | data formatting | bytes 4194304
  42.1 0.0 copy-done
  42.1 0.6 %copy.7 = f32[256]{0:T(256)} copy(f32[256]{0:T(256)S(1)} %bitcast.1) | data formatting | bytes 2048
Async XLA Ops:
  40.7 1.3 %copy-start = (f32[1,256]{1,0:T(1,128)S(1)}, f32[1,256]{1,0:T(1,128)}, u32[]{:S(2)}) copy-start(f32[1,256]{1,0:T(1,128)} %get-tuple-element.5) | copy-start | bytes 3076
